TPU v7x, 32 devices: a whole 2x2x4 slice. The times are simulated.
32 devices in a mesh: shard: 2 (over core), model: 4 (over y, x), unit: 4 (over z).
Axes of the slice: x: 2, y: 2, z: 4, core: 2. Of those that a mesh axis runs over, the one named last changes fastest.
Arguments:
- train_query: bfloat16 [16384, 4096], P(('unit', 'shard'), 'model'), parts along dimension 0, may hold values from -0.125 to 0.125
- low_query: bfloat16 [16384, 16], P(('unit', 'shard')), parts along dimension 0, may hold values from -0.09375 to 0.09375
- high_query: bfloat16 [64, 4096], P('unit', 'model'), parts along dimension 0, may hold values from -1.5 to 1.5
- train_key: bfloat16 [16384, 1024], P(('unit', 'shard'), 'model'), parts along dimension 0, may hold values from -0.125 to 0.125
- low_key: bfloat16 [16384, 16], P(('unit', 'shard')), parts along dimension 0, may hold values from -0.09375 to 0.09375
- high_key: bfloat16 [64, 1024], P('unit', 'model'), parts along dimension 0, may hold values from -1.5 to 1.5
- train_value: bfloat16 [16384, 1024], P(('unit', 'shard'), 'model'), parts along dimension 0, may hold values from -0.125 to 0.125
- low_value: bfloat16 [16384, 16], P(('unit', 'shard')), parts along dimension 0, may hold values from -0.09375 to 0.09375
- high_value: bfloat16 [64, 1024], P('unit', 'model'), parts along dimension 0, may hold values from -1.5 to 1.5
- norm_train: float32 [16384], P(('unit', 'shard', 'model')), parts along dimension 0, may hold values from 0.25 to 1.75
- norm_step: float32 [16384], P(('unit', 'shard', 'model')), parts along dimension 0, may hold values from -0.3 to 0.3
Outputs:
- serving_query: bfloat16 [16384, 4096], P('unit', 'model'), parts along dimension 0
- serving_key: bfloat16 [16384, 1024], P('unit', 'model'), parts along dimension 0
- serving_value: bfloat16 [16384, 1024], P('unit', 'model'), parts along dimension 0
- scale_query: float32 [16384], P(('unit', 'model')), parts along dimension 0
- scale_key: float32 [4096], P(('unit', 'model')), parts along dimension 0
- scale_value: float32 [4096], P(('unit', 'model')), parts along dimension 0
- serve_norm: bfloat16 [16384], P('unit'), parts along dimension 0
There are 4 independent parts, one for each index of `unit`. A program takes and returns all parts, laid end to end along the dimension named above; each array names one. Nothing has to cross between parts.
All inputs are finite; a program needn't handle non-finite values. Where the computation divides by a largest or mean magnitude, that divisor is 1e-20 or more.
Results may differ from a plain program's by a relative error of at most 0.001.
Values may be sent and summed in bfloat16 or wider, within the bound.
A program may use at most 64 MiB of HBM per device.

v0:
```python
import jax
import jax.numpy as jnp
from jax import lax
from jax.sharding import PartitionSpec as P

mix_rate = 1.0


def local(
    train_query,
    low_query,
    high_query,
    train_key,
    low_key,
    high_key,
    train_value,
    low_value,
    high_value,
    norm_train,
    norm_step,
):
    whole_query = train_query.astype(jnp.float32) + mix_rate * jnp.dot(
        low_query, high_query, preferred_element_type=jnp.float32
    )
    whole_key = train_key.astype(jnp.float32) + mix_rate * jnp.dot(
        low_key, high_key, preferred_element_type=jnp.float32
    )
    whole_value = train_value.astype(jnp.float32) + mix_rate * jnp.dot(
        low_value, high_value, preferred_element_type=jnp.float32
    )
    scale_query, scale_key, scale_value = lax.pmax(
        (
            jnp.max(jnp.abs(whole_query), axis=0),
            jnp.max(jnp.abs(whole_key), axis=0),
            jnp.max(jnp.abs(whole_value), axis=0),
        ),
        "shard",
    )
    narrow_query, narrow_key, narrow_value = (
        (whole_query / scale_query).astype(jnp.bfloat16),
        (whole_key / scale_key).astype(jnp.bfloat16),
        (whole_value / scale_value).astype(jnp.bfloat16),
    )
    serving_query, serving_key, serving_value = (
        lax.all_gather(narrow_query, "shard", axis=0, tiled=True),
        lax.all_gather(narrow_key, "shard", axis=0, tiled=True),
        lax.all_gather(narrow_value, "shard", axis=0, tiled=True),
    )
    serve_norm = lax.all_gather(
        (norm_train + norm_step).astype(jnp.bfloat16), ("shard", "model"), axis=0, tiled=True
    )
    return (
        serving_query,
        serving_key,
        serving_value,
        scale_query,
        scale_key,
        scale_value,
        serve_norm,
    )


def solution(mesh):
    in_specs = (
        P(("unit", "shard"), "model"),
        P(("unit", "shard"), None),
        P("unit", "model"),
        P(("unit", "shard"), "model"),
        P(("unit", "shard"), None),
        P("unit", "model"),
        P(("unit", "shard"), "model"),
        P(("unit", "shard"), None),
        P("unit", "model"),
        P(("unit", "shard", "model")),
        P(("unit", "shard", "model")),
    )
    out_specs = (
        P("unit", "model"),
        P("unit", "model"),
        P("unit", "model"),
        P(("unit", "model")),
        P(("unit", "model")),
        P(("unit", "model")),
        P("unit"),
    )
    return jax.shard_map(local, mesh=mesh, in_specs=in_specs, out_specs=out_specs, check_vma=False)
```

profile of v0, /device:TPU:0, one launch (start us, length us, event | category | flops | bytes accessed | tf_op | source)
XLA Modules:
  0.0 89.3 jit_solution(11863894634130557555)
XLA Ops:
  7.2 0.0 copy-start
  7.2 0.0 copy-start.7
  7.2 0.0 all-gather.7.cloned.1.call-start
  7.3 0.0 copy-start.1
  7.3 3.2 %abs_reduce_fusion.2 = (f32[256]{0:T(256)S(1)}, f32[2048,256]{1,0:T(8,128)}) fusion(bf16[2048,16]{0,1:T(8,128)(2,1)} %param.15, bf16[16,256]{1,0:T(8,128)(2,1)} %param.16, bf16[2048,256]{1,0:T(8,128)(2,1)} %param.14), kind=kOutput, calls=%fused_computation.8 | convolution fusion | flops 18874112 | bytes 3220480 | tf_op jit(solution)/shard_map/dot_general | solution.py:25
  10.5 0.0 copy-done.5
  10.5 0.0 copy-start.6
  10.5 0.5 abs_reduce_fusion.1
  11.1 0.0 copy-done
  11.1 0.0 copy-done.1
  11.1 0.2 copy-done.6
  11.3 4.7 %abs_reduce_fusion = (f32[1024]{0:T(1024)S(1)}, f32[2048,1024]{1,0:T(8,128)}) fusion(bf16[2048,1024]{1,0:T(8,128)(2,1)S(1)} %copy-done.1, bf16[2048,16]{0,1:T(8,128)(2,1)S(1)} %copy-done, bf16[16,1024]{1,0:T(8,128)(2,1)S(1)} %copy-done.6), kind=kOutput, calls=%fused_computation.1 | convolution fusion | flops 75496448 | bytes 12685312 | tf_op jit(solution)/shard_map/dot_general | solution.py:22
  15.9 2.6 %all-reduce = (f32[1024]{0:T(1024)S(1)}, f32[256]{0:T(256)S(1)}, f32[256]{0:T(256)S(1)}) all-reduce(f32[1024]{0:T(1024)S(1)} %get-tuple-element.10, f32[256]{0:T(256)S(1)} %get-tuple-element.12, f32[256]{0:T(256)S(1)} %get-tuple-element.14), channel_id=1, replica_groups=mesh['shard'=2,'model'=4,'unit'=4] {'shard'}, use_global_device_ids=true, to_apply=%region_1.0 | all-reduce | flops 1536 | bytes 12288 | tf_op jit(solution)/shard_map/pmax | solution.py:31
  18.6 0.0 copy-start.8
  18.6 2.7 %divide_convert_fusion.2 = bf16[2048,256]{1,0:T(8,128)(2,1)} fusion(f32[2048,256]{1,0:T(8,128)} %get-tuple-element.13, f32[256]{0:T(256)S(1)} %get-tuple-element.27), kind=kLoop, calls=%fused_computation.7 | loop fusion | flops 1048576 | bytes 3146752 | tf_op jit(solution)/shard_map/convert_element_type | solution.py:41
  21.3 0.0 all-gather.7.cloned.1.call-update
  21.3 0.0 copy-done.11
  21.3 0.0 all-gather.9.cloned.1.call-start
  21.4 1.1 %divide_convert_fusion.1 = bf16[2048,256]{1,0:T(8,128)(2,1)} fusion(f32[2048,256]{1,0:T(8,128)S(1)} %get-tuple-element.15, f32[256]{0:T(256)S(1)} %get-tuple-element.28), kind=kLoop, calls=%fused_computation.5 | loop fusion | flops 1048576 | bytes 3146752 | tf_op jit(solution)/shard_map/convert_element_type | solution.py:42
  22.5 0.0 all-gather.9.cloned.1.call-update
  22.6 0.0 all-gather.5.cloned.1.call-start
  22.6 8.1 %divide_convert_fusion = bf16[2048,1024]{1,0:T(8,128)(2,1)} fusion(f32[2048,1024]{1,0:T(8,128)} %get-tuple-element.11, bf16[2048,1024]{1,0:T(8,128)(2,1)} %param.11, f32[1024]{0:T(1024)S(1)} %get-tuple-element.26), kind=kLoop, calls=%fused_computation | loop fusion | flops 8388608 | bytes 16781312 | tf_op jit(solution)/shard_map/convert_element_type | solution.py:40
  30.7 0.0 all-gather.5.cloned.1.call-update
  30.8 0.7 copy-done.9
  31.4 0.0 copy-done.10
  31.5 20.5 %all-gather = bf16[8,1,512]{2,1,0:T(2,128)(2,1)S(1)} all-gather(bf16[1,1,512]{2,1,0:T(2,128)(2,1)S(1)} %reshape.17), channel_id=1, replica_groups=mesh['shard'=2,'model'=4,'unit'=4] {'shard','model'}, dimensions={0}, use_global_device_ids=true | all-gather | bytes 9216 | tf_op jit(solution)/shard_map/all_gather | solution.py:49
  52.0 0.6 copy.18
  52.6 18.6 %all-gather.5.cloned.1.call-done = bf16[4096,1024]{1,0:T(8,128)(2,1)} async-done(((bf16[2048,1024]{1,0:T(8,128)(2,1)}), bf16[4096,1024]{1,0:T(8,128)(2,1)}) %all-gather.5.cloned.1.call-update) | async-done | bytes 8388624 | tf_op jit(solution)/shard_map/all_gather | solution.py:45
  71.1 7.9 %copy.22 = bf16[4096,1024]{1,0:T(8,128)(2,1)} copy(bf16[4096,1024]{1,0:T(8,128)(2,1)} %all-gather.5.cloned.1.call-done) | data formatting | bytes 16777216
  79.1 1.3 %copy.23 = bf16[4096,256]{1,0:T(8,128)(2,1)} copy(bf16[4096,256]{1,0:T(8,128)(2,1)S(1)} %copy-done.2) | data formatting | bytes 4194304
  80.4 1.0 %copy-done.3 = bf16[4096,256]{1,0:T(8,128)(2,1)S(1)} copy-done((bf16[4096,256]{1,0:T(8,128)(2,1)S(1)}, bf16[4096,256]{1,0:T(8,128)(2,1)}, u32[]{:S(2)}) %copy-start.3) | copy-done | bytes 2097176
  81.4 1.3 %copy.24 = bf16[4096,256]{1,0:T(8,128)(2,1)} copy(bf16[4096,256]{1,0:T(8,128)(2,1)S(1)} %copy-done.3) | data formatting | bytes 4194304
  (18 shorter events, 0.1 us)
Async XLA Ops:
  7.2 3.9 %copy-start = (bf16[2048,16]{0,1:T(8,128)(2,1)S(1)}, bf16[2048,16]{0,1:T(8,128)(2,1)}, u32[]{:S(2)}) copy-start(bf16[2048,16]{0,1:T(8,128)(2,1)} %param.12) | copy-start | bytes 196612
  7.2 3.3 %copy-start.7 = (bf16[16,256]{1,0:T(8,128)(2,1)S(1)}, bf16[16,256]{1,0:T(8,128)(2,1)}, u32[]{:S(2)}) copy-start(bf16[16,256]{1,0:T(8,128)(2,1)} %param.19) | copy-start | bytes 24580
  7.2 3.3 %copy-start.5 = (bf16[2048,16]{0,1:T(8,128)(2,1)S(1)}, bf16[2048,16]{0,1:T(8,128)(2,1)}, u32[]{:S(2)}) copy-start(bf16[2048,16]{0,1:T(8,128)(2,1)} %param.18) | copy-start | bytes 196612
  7.2 3.3 %copy-start.4 = (bf16[2048,256]{1,0:T(8,128)(2,1)S(1)}, bf16[2048,256]{1,0:T(8,128)(2,1)}, u32[]{:S(2)}) copy-start(bf16[2048,256]{1,0:T(8,128)(2,1)} %param.17) | copy-start | bytes 3145732
  7.2 45.4 %all-gather.7.cloned.1.call-start = ((), (), s32[]{:S(2)}) async-start(), calls=%async_computation.1 | async-start | bytes 3145728 | tf_op jit(solution)/shard_map/all_gather | solution.py:46
  7.3 3.8 %copy-start.1 = (bf16[2048,1024]{1,0:T(8,128)(2,1)S(1)}, bf16[2048,1024]{1,0:T(8,128)(2,1)}, u32[]{:S(2)}) copy-start(bf16[2048,1024]{1,0:T(8,128)(2,1)} %param.11) | copy-start | bytes 12582916
  10.5 0.8 copy-start.6
  18.6 2.8 %copy-start.11 = (f32[256]{0:T(256)}, f32[256]{0:T(256)S(1)}, u32[]{:S(2)}) copy-start(f32[256]{0:T(256)S(1)} %get-tuple-element.27) | copy-start | bytes 3076
  18.6 2.8 %copy-start.12 = (f32[256]{0:T(256)}, f32[256]{0:T(256)S(1)}, u32[]{:S(2)}) copy-start(f32[256]{0:T(256)S(1)} %get-tuple-element.28) | copy-start | bytes 3076
  18.6 4.0 %copy-start.8 = (f32[1024]{0:T(1024)}, f32[1024]{0:T(1024)S(1)}, u32[]{:S(2)}) copy-start(f32[1024]{0:T(1024)S(1)} %get-tuple-element.26) | copy-start | bytes 12292
  21.3 31.2 %all-gather.9.cloned.1.call-start = ((), (), s32[]{:S(2)}) async-start(), calls=%async_computation.2 | async-start | bytes 3145728 | tf_op jit(solution)/shard_map/all_gather | solution.py:47
  22.6 48.6 %all-gather.5.cloned.1.call-start = ((), (), s32[]{:S(2)}) async-start(), calls=%async_computation | async-start | bytes 12582912 | tf_op jit(solution)/shard_map/all_gather | solution.py:45
  30.7 0.7 copy-start.9
  30.7 0.7 copy-start.10
  71.1 7.9 %copy-start.2 = (bf16[4096,256]{1,0:T(8,128)(2,1)S(1)}, bf16[4096,256]{1,0:T(8,128)(2,1)}, u32[]{:S(2)}) copy-start(bf16[4096,256]{1,0:T(8,128)(2,1)} %all-gather.7.cloned.1.call-done) | copy-start | bytes 6291460
  79.1 2.3 %copy-start.3 = (bf16[4096,256]{1,0:T(8,128)(2,1)S(1)}, bf16[4096,256]{1,0:T(8,128)(2,1)}, u32[]{:S(2)}) copy-start(bf16[4096,256]{1,0:T(8,128)(2,1)} %all-gather.9.cloned.1.call-done) | copy-start | bytes 6291460
Sparse Core Ops, SparseCore 0:
  21.5 13.1 all-gather.6
  36.8 11.7 all-gather.8
  50.1 21.0 all-gather.4
where the time goes:
time: 89.6 us; the launch traced here: 89.3 us
  blocking collectives  23.1 us (26%)
  waiting for transfers between devices  18.6 us (21%)
  between operations  13.9 us (16%)
  local copies, waits for them, and re-layouts  13.1 us (15%)
  other arithmetic  12 us (13%)
  matrix products  8.44 us (9%)
    all_gather x1, blocking collectives, local(): lax.all_gather((norm_train + norm_step).astype(jnp.bfloat16), ('shard', '...  20.5 us
    all_gather x1, waiting for transfers between devices, local(): lax.all_gather(narrow_query, 'shard', axis=0, tiled=True)  18.6 us
    unnamed x31, local copies, waits for them, and re-layouts  13.1 us
    convert_element_type x1, other arithmetic, local(): (whole_query / scale_query).astype(jnp.bfloat16)  8.11 us
    dot_general x1, matrix products, local(): jnp.dot(low_query, high_query, preferred_element_type=jnp.float32)  4.68 us
    dot_general x1, matrix products, local(): jnp.dot(low_key, high_key, preferred_element_type=jnp.float32)  3.22 us
    convert_element_type x1, other arithmetic, local(): (whole_key / scale_key).astype(jnp.bfloat16)  2.73 us
    pmax x1, blocking collectives, local(): lax.pmax((jnp.max(jnp.abs(whole_query), axis=0), jnp.max(jnp.abs(whole_ke...  2.62 us
  transfers between devices with their start and end apart: 3, of which 1 were waited for; matrix products, arithmetic and copies ran while one was open for 11% of the time, Pallas kernels for 0%

commit v1 on v0

v1 whole, which is shorter than its diff:
```python
import functools

import jax
import jax.numpy as jnp
from jax import lax
from jax.experimental import pallas as pl
from jax.experimental.pallas import tpu as pltpu
from jax.sharding import PartitionSpec as P

mix_rate = 1.0
MESH = pl.DeviceIdType.MESH
MIB = 1 << 20


def exchange_kernel(
    n_shard,
    n_model,
    chunks,
    tile,
    tq, lq, hq, tk, lk, hk, tv, lv, hv, nt, ns,
    wq, wk, wv, sq, sk, sv, norm,
    base, low_q, low_k, low_v, high_q, high_k, high_v, norms,
    send_base, recv_base, send_low, recv_low, local_high, send_norm, recv_norm,
):
    trains, lows, highs = (tq, tk, tv), (lq, lk, lv), (hq, hk, hv)
    low_bufs, high_bufs = (low_q, low_k, low_v), (high_q, high_k, high_v)
    wholes, scales = (wq, wk, wv), (sq, sk, sv)
    rows = tq.shape[0]
    shard, model = lax.axis_index("shard"), lax.axis_index("model")
    group = n_shard * n_model
    place = shard * n_model + model

    local = []
    for i in (1, 2, 0):
        local.append(pltpu.make_async_copy(lows[i], low_bufs[i].at[0], recv_low.at[0, i]))
        local.append(pltpu.make_async_copy(highs[i], high_bufs[i], local_high.at[i]))
    for c, (i, start, width) in enumerate(chunks):
        local.append(
            pltpu.make_async_copy(
                trains[i].at[:, pl.ds(start, width)], base.at[0, c], recv_base.at[0, c]
            )
        )
    local.append(pltpu.make_async_copy(nt, norms.at[place, 0], recv_norm.at[0, 0]))
    local.append(pltpu.make_async_copy(ns, norms.at[place, 1], recv_norm.at[0, 1]))

    barrier = pltpu.get_barrier_semaphore()
    for k in range(1, group):
        other = lax.rem(place + k, group)
        pl.semaphore_signal(
            barrier, inc=1,
            device_id={"shard": other // n_model, "model": lax.rem(other, n_model)},
            device_id_type=MESH,
        )
    for copy in local:
        copy.start()
    pl.semaphore_wait(barrier, group - 1)

    sends_low, sends_base, sends_norm = {}, {}, {}
    for d in range(1, n_shard):
        to = {"shard": lax.rem(shard + d, n_shard)}
        for i in (1, 2, 0):
            sends_low[d, i] = pltpu.make_async_remote_copy(
                src_ref=lows[i], dst_ref=low_bufs[i].at[d],
                send_sem=send_low.at[d, i], recv_sem=recv_low.at[d, i],
                device_id=to, device_id_type=MESH,
            )
            sends_low[d, i].start()
    for c, (i, start, width) in enumerate(chunks):
        for d in range(1, n_shard):
            to = {"shard": lax.rem(shard + d, n_shard)}
            sends_base[d, c] = pltpu.make_async_remote_copy(
                src_ref=trains[i].at[:, pl.ds(start, width)], dst_ref=base.at[d, c],
                send_sem=send_base.at[d, c], recv_sem=recv_base.at[d, c],
                device_id=to, device_id_type=MESH,
            )
            sends_base[d, c].start()
    for k in range(1, group):
        other = lax.rem(place + k, group)
        to = {"shard": other // n_model, "model": lax.rem(other, n_model)}
        for j, source in enumerate((nt, ns)):
            sends_norm[k, j] = pltpu.make_async_remote_copy(
                src_ref=source, dst_ref=norms.at[place, j],
                send_sem=send_norm.at[k, j], recv_sem=recv_norm.at[k, j],
                device_id=to, device_id_type=MESH,
            )
            sends_norm[k, j].start()

    for copy in local:
        copy.wait()

    def merge(d, c):
        i, start, width = chunks[c]
        first = lax.rem(shard - d + n_shard, n_shard) * rows
        high = high_bufs[i][:, start:start + width]

        def step(t, top):
            at = pl.multiple_of(t * tile, tile)
            product = lax.dot_general(
                low_bufs[i][d, :, pl.ds(at, tile)], high,
                (((0,), (0,)), ((), ())), preferred_element_type=jnp.float32,
            )
            whole = base[d, c, pl.ds(at, tile), :].astype(jnp.float32) + mix_rate * product
            wholes[i][pl.ds(pl.multiple_of(first + at, tile), tile), start:start + width] = whole
            return jnp.maximum(top, jnp.max(jnp.abs(whole).reshape(tile // 8, 8, width), axis=0))

        return lax.fori_loop(0, rows // tile, step, jnp.zeros((8, width), jnp.float32))

    tops = [merge(0, c) for c in range(len(chunks))]
    for d in range(1, n_shard):
        for i in (1, 2, 0):
            sends_low[d, i].wait()
    for c, (i, start, width) in enumerate(chunks):
        for d in range(1, n_shard):
            sends_base[d, c].wait()
            tops[c] = jnp.maximum(tops[c], merge(d, c))
        scales[i][:, start:start + width] = jnp.max(tops[c], axis=0, keepdims=True)
    for k in range(1, group):
        for j in range(2):
            sends_norm[k, j].wait()
    norm[...] = (norms[:, 0] + norms[:, 1]).reshape(norm.shape).astype(norm.dtype)


def scale_kernel(
    plan,
    wq, wk, wv, sq, sk, sv, norm,
    oq, ok, ov, osq, osk, osv, onorm,
    buf_q, buf_k, buf_v, sems,
):
    wholes, scales = (wq, wk, wv), (sq, sk, sv)
    outs, bufs = (oq, ok, ov), (buf_q, buf_k, buf_v)
    for source, target in ((sq, osq), (sk, osk), (sv, osv), (norm, onorm)):
        target[...] = source[...]
    for i, step, count, base in plan:
        inverse = 1.0 / scales[i][...]

        def copy(t):
            at = pl.multiple_of(t * step, step)
            return pltpu.make_async_copy(
                bufs[i].at[pl.ds(at, step), :], outs[i].at[pl.ds(at, step), :], sems.at[base + t]
            )

        @pl.loop(0, count)
        def _(t):
            at = pl.multiple_of(t * step, step)
            bufs[i][pl.ds(at, step), :] = (wholes[i][pl.ds(at, step), :] * inverse).astype(bufs[i].dtype)
            copy(t).start()

    for i, step, count, base in plan:
        @pl.loop(0, count)
        def _(t):
            at = pl.multiple_of(t * step, step)
            pltpu.make_async_copy(
                bufs[i].at[pl.ds(at, step), :], outs[i].at[pl.ds(at, step), :], sems.at[base + t]
            ).wait()


def local(n_shard, n_model, tq, lq, hq, tk, lk, hk, tv, lv, hv, nt, ns):
    rows, rank = tq.shape[0], hq.shape[0]
    widths = (tq.shape[1], tk.shape[1], tv.shape[1])
    width = min(min(widths), 256)
    tile = min(rows, 256)
    chunks = tuple((i, s, width) for i in (1, 2, 0) for s in range(0, widths[i], width))
    group = n_shard * n_model
    lanes = 128 if nt.shape[0] % 128 == 0 else nt.shape[0]
    piece = (nt.shape[0] // lanes, lanes)
    full = n_shard * rows
    f32, bf16 = jnp.float32, jnp.bfloat16
    dma = pltpu.SemaphoreType.DMA
    hbm, vmem = pl.BlockSpec(memory_space=pltpu.HBM), pl.BlockSpec(memory_space=pltpu.VMEM)
    norm_shape = (group * piece[0], lanes)

    parts = pl.pallas_call(
        functools.partial(exchange_kernel, n_shard, n_model, chunks, tile),
        out_shape=[pltpu.VMEM((full, w), f32) for w in widths]
        + [pltpu.VMEM((1, w), f32) for w in widths]
        + [pltpu.VMEM(norm_shape, bf16)],
        in_specs=[hbm] * 11,
        out_specs=[vmem] * 7,
        scratch_shapes=[pltpu.VMEM((n_shard, len(chunks), rows, width), bf16)]
        + [pltpu.VMEM((n_shard, rank, rows), bf16)] * 3
        + [pltpu.VMEM((rank, w), bf16) for w in widths]
        + [
            pltpu.VMEM((group, 2) + piece, f32),
            dma((n_shard, len(chunks))), dma((n_shard, len(chunks))),
            dma((n_shard, 3)), dma((n_shard, 3)), dma((3,)),
            dma((group, 2)), dma((group, 2)),
        ],
        compiler_params=pltpu.CompilerParams(
            collective_id=0, has_side_effects=True, vmem_limit_bytes=18 * MIB
        ),
        cost_estimate=pl.CostEstimate(flops=0, bytes_accessed=40 * MIB, transcendentals=0),
        name="exchange",
    )(*(pltpu.with_memory_space_constraint(x, pltpu.HBM) for x in (tq, lq.T, hq, tk, lk.T, hk, tv, lv.T, hv, nt.reshape(piece), ns.reshape(piece))))

    plan, base = [], 0
    for i in (0, 1, 2):
        step = min(full, 256 * max(widths) // widths[i])
        plan.append((i, step, full // step, base))
        base += full // step
    outs = pl.pallas_call(
        functools.partial(scale_kernel, tuple(plan)),
        out_shape=[jax.ShapeDtypeStruct((full, w), bf16) for w in widths]
        + [jax.ShapeDtypeStruct((1, w), f32) for w in widths]
        + [jax.ShapeDtypeStruct(norm_shape, bf16)],
        in_specs=[pl.BlockSpec(memory_space=pltpu.VMEM)] * 7,
        out_specs=[hbm] * 3 + [vmem] * 4,
        scratch_shapes=[pltpu.VMEM((full, w), bf16) for w in widths] + [dma((base,))],
        compiler_params=pltpu.CompilerParams(vmem_limit_bytes=18 * MIB),
        cost_estimate=pl.CostEstimate(flops=0, bytes_accessed=40 * MIB, transcendentals=0),
        name="scale",
    )(*(pltpu.with_memory_space_constraint(x, pltpu.VMEM) for x in parts))
    return (*outs[:3], *(o.reshape(-1) for o in outs[3:]))


def solution(mesh):
    in_specs = (
        P(("unit", "shard"), "model"),
        P(("unit", "shard"), None),
        P("unit", "model"),
        P(("unit", "shard"), "model"),
        P(("unit", "shard"), None),
        P("unit", "model"),
        P(("unit", "shard"), "model"),
        P(("unit", "shard"), None),
        P("unit", "model"),
        P(("unit", "shard", "model")),
        P(("unit", "shard", "model")),
    )
    out_specs = (
        P("unit", "model"),
        P("unit", "model"),
        P("unit", "model"),
        P(("unit", "model")),
        P(("unit", "model")),
        P(("unit", "model")),
        P("unit"),
    )
    body = functools.partial(local, mesh.shape["shard"], mesh.shape["model"])
    return jax.shard_map(body, mesh=mesh, in_specs=in_specs, out_specs=out_specs, check_vma=False)
```

time: 89.6 us -> 33.4 us (0.37)
  Pallas kernels: 0 us -> 32.6 us
  blocking collectives: 23.1 us -> 0 us
  waiting for transfers between devices: 18.6 us -> 0 us
  between operations: 13.9 us -> 0.64 us
  local copies, waits for them, and re-layouts: 13.1 us -> 0 us
  other arithmetic: 12 us -> 0 us
  matrix products: 8.44 us -> 0 us
    pallas_call x0 -> x2, Pallas kernels: none -> 32.6 us  [the longest x1 27.2 us: local(): pl.pallas_call(functools.partial(exchange_kernel, n_shard, n_model, chunk...]
    all_gather x1 -> x0, blocking collectives: 20.5 us -> none  [local(): lax.all_gather((norm_train + norm_step).astype(jnp.bfloat16), ('shard', '...]
    all_gather x3 -> x0, waiting for transfers between devices: 18.6 us -> none  [the longest x1 18.6 us: local(): lax.all_gather(narrow_query, 'shard', axis=0, tiled=True)]
    unnamed x31 -> x0, local copies, waits for them, and re-layouts: 13.1 us -> none
    convert_element_type x4 -> x0, other arithmetic: 12 us -> none  [the longest x1 8.11 us: local(): (whole_query / scale_query).astype(jnp.bfloat16)]
    dot_general x3 -> x0, matrix products: 8.44 us -> none  [the longest x1 4.68 us: local(): jnp.dot(low_query, high_query, preferred_element_type=jnp.float32)]
    pmax x1 -> x0, blocking collectives: 2.62 us -> none  [local(): lax.pmax((jnp.max(jnp.abs(whole_query), axis=0), jnp.max(jnp.abs(whole_ke...]
  transfers between devices with their start and end apart: 3 -> 0, of which waited for: 1 -> 0; matrix products, arithmetic and copies ran while one was open for 11% -> 0% of each run, Pallas kernels for 0% -> 0%
where the time goes in v1:
time: 33.4 us; the launch traced here: 33.3 us
  Pallas kernels  32.6 us (98%)
  between operations  0.64 us (2%)
    pallas_call x1, Pallas kernels, local(): pl.pallas_call(functools.partial(exchange_kernel, n_shard, n_model, chunk...  27.2 us
    pallas_call x1, Pallas kernels, local(): pl.pallas_call(functools.partial(scale_kernel, tuple(plan)), out_shape=[j...  5.42 us

profile of v1, /device:TPU:0, one launch (start us, length us, event | category | flops | bytes accessed | tf_op | source)
XLA Modules:
  0.0 33.3 jit_solution(2569428342778178492)
XLA Ops:
  0.6 27.2 %exchange.1 = (f32[4096,1024]{1,0:T(8,128)S(1)}, f32[4096,256]{1,0:T(8,128)S(1)}, f32[4096,256]{1,0:T(8,128)S(1)}, f32[1,1024]{1,0:T(1,128)S(1)}, f32[1,256]{1,0...) custom-call(bf16[2048,1024]{1,0:T(8,128)(2,1)} %tq.1, bf16[16,2048]{1,0:T(8,128)(2,1)} %bitcast.9, ...), custom_call_target="tpu_custom_call" | custom-call | bytes 41943040 | tf_op jit(solution)/shard_map/exchange/pallas_call | solution.py:172
  27.8 5.4 %scale.1 = (bf16[4096,1024]{1,0:T(8,128)(2,1)}, bf16[4096,256]{1,0:T(8,128)(2,1)}, bf16[4096,256]{1,0:T(8,128)(2,1)}, f32[1,1024]{1,0:T(1,128)}, f32[1,256]{1,0:...) custom-call(f32[4096,1024]{1,0:T(8,128)S(1)} %get-tuple-element.21.wq, f32[4096,256]{1,0:T(8,128)S(1)} %get-tuple-element.22.wk, ...), custom_call_target="tpu_custom_call" | custom-call | bytes 41943040 | tf_op jit(solution)/shard_map/scale/pallas_call | solution.py:200

commit v2 on v1

v2 whole, which is shorter than its diff:
```python
import functools

import jax
import jax.numpy as jnp
from jax import lax
from jax.experimental import pallas as pl
from jax.experimental.pallas import tpu as pltpu
from jax.sharding import PartitionSpec as P

mix_rate = 1.0
MESH = pl.DeviceIdType.MESH
MIB = 1 << 20


def exchange_kernel(
    n_shard,
    n_model,
    tile,
    tq, lq, hq, tk, lk, hk, tv, lv, hv, nt, ns,
    wq, wk, wv, sq, sk, sv, norm,
    base_q, base_k, base_v, low_q, low_k, low_v, high_q, high_k, high_v, norms,
    send_base, recv_base, send_low, recv_low, local_high, send_norm, recv_norm,
):
    trains, lows, highs = (tq, tk, tv), (lq, lk, lv), (hq, hk, hv)
    bases, low_bufs, high_bufs = (base_q, base_k, base_v), (low_q, low_k, low_v), (high_q, high_k, high_v)
    wholes, scales = (wq, wk, wv), (sq, sk, sv)
    rows = tq.shape[0]
    steps = rows // tile
    shard, model = lax.axis_index("shard"), lax.axis_index("model")
    group = n_shard * n_model
    place = shard * n_model + model

    barrier = pltpu.get_barrier_semaphore()
    for k in range(1, group):
        other = lax.rem(place + k, group)
        pl.semaphore_signal(
            barrier, inc=1,
            device_id={"shard": other // n_model, "model": lax.rem(other, n_model)},
            device_id_type=MESH,
        )

    def own_base(t, i):
        at = pl.ds(t * tile, tile)
        return pltpu.make_async_copy(trains[i].at[at, :], bases[i].at[0, at, :], recv_base.at[0, t, i])

    local = []
    for i in range(3):
        local.append(pltpu.make_async_copy(lows[i], low_bufs[i].at[0], recv_low.at[0, i]))
        local.append(pltpu.make_async_copy(highs[i], high_bufs[i], local_high.at[i]))
    for copy in local:
        copy.start()
    for t in range(steps):
        for i in range(3):
            own_base(t, i).start()
    own_norm = [
        pltpu.make_async_copy(source, norms.at[place, j], recv_norm.at[0, j])
        for j, source in enumerate((nt, ns))
    ]
    for copy in own_norm:
        copy.start()
    pl.semaphore_wait(barrier, group - 1)

    def low_copy(d, i):
        return pltpu.make_async_remote_copy(
            src_ref=lows[i], dst_ref=low_bufs[i].at[d],
            send_sem=send_low.at[d, i], recv_sem=recv_low.at[d, i],
            device_id={"shard": lax.rem(shard + d, n_shard)}, device_id_type=MESH,
        )

    def base_copy(d, t, i):
        at = pl.ds(t * tile, tile)
        return pltpu.make_async_remote_copy(
            src_ref=trains[i].at[at, :], dst_ref=bases[i].at[d, at, :],
            send_sem=send_base.at[d, t, i], recv_sem=recv_base.at[d, t, i],
            device_id={"shard": lax.rem(shard + d, n_shard)}, device_id_type=MESH,
        )

    def norm_copy(k, j):
        other = lax.rem(place + k, group)
        return pltpu.make_async_remote_copy(
            src_ref=(nt, ns)[j], dst_ref=norms.at[place, j],
            send_sem=send_norm.at[k, j], recv_sem=recv_norm.at[k, j],
            device_id={"shard": other // n_model, "model": lax.rem(other, n_model)},
            device_id_type=MESH,
        )

    for d in range(1, n_shard):
        for i in range(3):
            low_copy(d, i).start()
    for t in range(steps):
        for d in range(1, n_shard):
            for i in range(3):
                base_copy(d, t, i).start()
    for k in range(1, group):
        for j in range(2):
            norm_copy(k, j).start()

    def merge(d, t, tops):
        first = lax.rem(shard - d + n_shard, n_shard) * rows
        at = pl.multiple_of(t * tile, tile)
        to = pl.multiple_of(first + at, tile)
        new = []
        for i in range(3):
            top = tops[i]
            product = lax.dot_general(
                low_bufs[i][d, :, pl.ds(at, tile)], high_bufs[i][...],
                (((0,), (0,)), ((), ())), preferred_element_type=jnp.float32,
            )
            whole = bases[i][d, pl.ds(at, tile), :].astype(jnp.float32) + mix_rate * product
            wholes[i][pl.ds(to, tile), :] = whole
            top = jnp.maximum(top, jnp.max(jnp.abs(whole).reshape(tile // 8, 8, whole.shape[1]), axis=0))
            new.append(top)
        return tuple(new)

    tops = tuple(jnp.zeros((8, h.shape[1]), jnp.float32) for h in high_bufs)
    for copy in local:
        copy.wait()

    def own_step(t, tops):
        for i in range(3):
            own_base(t, i).wait()
        return merge(0, t, tops)

    tops = lax.fori_loop(0, steps, own_step, tops)
    for d in range(1, n_shard):
        for i in range(3):
            low_copy(d, i).wait()

    def other_step(u, tops):
        t, d = u // (n_shard - 1), 1 + lax.rem(u, n_shard - 1)
        for i in range(3):
            base_copy(d, t, i).wait()
        return merge(d, t, tops)

    tops = lax.fori_loop(0, steps * (n_shard - 1), other_step, tops)
    for i in range(3):
        scales[i][...] = jnp.max(tops[i], axis=0, keepdims=True)
    for copy in own_norm:
        copy.wait()
    for k in range(1, group):
        for j in range(2):
            norm_copy(k, j).wait()
    norm[...] = (norms[:, 0] + norms[:, 1]).reshape(norm.shape).astype(norm.dtype)


def scale_kernel(
    plan,
    wq, wk, wv, sq, sk, sv, norm,
    oq, ok, ov, osq, osk, osv, onorm,
    buf_q, buf_k, buf_v, sems, small_sems,
):
    wholes, scales = (wq, wk, wv), (sq, sk, sv)
    outs, bufs = (oq, ok, ov), (buf_q, buf_k, buf_v)
    small = [
        pltpu.make_async_copy(source, target, small_sems.at[n])
        for n, (source, target) in enumerate(((sq, osq), (sk, osk), (sv, osv), (norm, onorm)))
    ]
    for copy in small:
        copy.start()
    for i, step, count, base in plan:
        inverse = 1.0 / scales[i][...]

        def copy(t):
            at = pl.multiple_of(t * step, step)
            return pltpu.make_async_copy(
                bufs[i].at[pl.ds(at, step), :], outs[i].at[pl.ds(at, step), :], sems.at[base + t]
            )

        @pl.loop(0, count)
        def _(t):
            at = pl.multiple_of(t * step, step)
            bufs[i][pl.ds(at, step), :] = (wholes[i][pl.ds(at, step), :] * inverse).astype(bufs[i].dtype)
            copy(t).start()

    for i, step, count, base in plan:
        @pl.loop(0, count)
        def _(t):
            at = pl.multiple_of(t * step, step)
            pltpu.make_async_copy(
                bufs[i].at[pl.ds(at, step), :], outs[i].at[pl.ds(at, step), :], sems.at[base + t]
            ).wait()
    for copy in small:
        copy.wait()


def local(n_shard, n_model, tq, lq, hq, tk, lk, hk, tv, lv, hv, nt, ns):
    rows, rank = tq.shape[0], hq.shape[0]
    widths = (tq.shape[1], tk.shape[1], tv.shape[1])
    tile = min(rows, 256)
    steps = rows // tile
    group = n_shard * n_model
    lanes = 128 if nt.shape[0] % 128 == 0 else nt.shape[0]
    piece = (nt.shape[0] // lanes, lanes)
    full = n_shard * rows
    f32, bf16 = jnp.float32, jnp.bfloat16
    dma = pltpu.SemaphoreType.DMA
    hbm, vmem = pl.BlockSpec(memory_space=pltpu.HBM), pl.BlockSpec(memory_space=pltpu.VMEM)
    norm_shape = (group * piece[0], lanes)

    parts = pl.pallas_call(
        functools.partial(exchange_kernel, n_shard, n_model, tile),
        out_shape=[pltpu.VMEM((full, w), f32) for w in widths]
        + [pltpu.VMEM((1, w), f32) for w in widths]
        + [pltpu.VMEM(norm_shape, bf16)],
        in_specs=[hbm] * 11,
        out_specs=[vmem] * 7,
        scratch_shapes=[pltpu.VMEM((n_shard, rows, w), bf16) for w in widths]
        + [pltpu.VMEM((n_shard, rank, rows), bf16)] * 3
        + [pltpu.VMEM((rank, w), bf16) for w in widths]
        + [
            pltpu.VMEM((group, 2) + piece, f32),
            dma((n_shard, steps, 3)), dma((n_shard, steps, 3)),
            dma((n_shard, 3)), dma((n_shard, 3)), dma((3,)),
            dma((group, 2)), dma((group, 2)),
        ],
        compiler_params=pltpu.CompilerParams(
            collective_id=0, has_side_effects=True, vmem_limit_bytes=18 * MIB
        ),
        cost_estimate=pl.CostEstimate(flops=0, bytes_accessed=40 * MIB, transcendentals=0),
        name="exchange",
    )(*(pltpu.with_memory_space_constraint(x, pltpu.HBM) for x in (tq, lq.T, hq, tk, lk.T, hk, tv, lv.T, hv, nt.reshape(piece), ns.reshape(piece))))

    plan, base = [], 0
    for i in (0, 1, 2):
        step = min(full, 256 * max(widths) // widths[i])
        plan.append((i, step, full // step, base))
        base += full // step
    outs = pl.pallas_call(
        functools.partial(scale_kernel, tuple(plan)),
        out_shape=[jax.ShapeDtypeStruct((full, w), bf16) for w in widths]
        + [jax.ShapeDtypeStruct((1, w), f32) for w in widths]
        + [jax.ShapeDtypeStruct(norm_shape, bf16)],
        in_specs=[pl.BlockSpec(memory_space=pltpu.VMEM)] * 7,
        out_specs=[hbm] * 7,
        scratch_shapes=[pltpu.VMEM((full, w), bf16) for w in widths] + [dma((base,)), dma((4,))],
        compiler_params=pltpu.CompilerParams(vmem_limit_bytes=18 * MIB),
        cost_estimate=pl.CostEstimate(flops=0, bytes_accessed=40 * MIB, transcendentals=0),
        name="scale",
    )(*(pltpu.with_memory_space_constraint(x, pltpu.VMEM) for x in parts))
    return (*outs[:3], *(o.reshape(-1) for o in outs[3:]))


def solution(mesh):
    in_specs = (
        P(("unit", "shard"), "model"),
        P(("unit", "shard"), None),
        P("unit", "model"),
        P(("unit", "shard"), "model"),
        P(("unit", "shard"), None),
        P("unit", "model"),
        P(("unit", "shard"), "model"),
        P(("unit", "shard"), None),
        P("unit", "model"),
        P(("unit", "shard", "model")),
        P(("unit", "shard", "model")),
    )
    out_specs = (
        P("unit", "model"),
        P("unit", "model"),
        P("unit", "model"),
        P(("unit", "model")),
        P(("unit", "model")),
        P(("unit", "model")),
        P("unit"),
    )
    body = functools.partial(local, mesh.shape["shard"], mesh.shape["model"])
    return jax.shard_map(body, mesh=mesh, in_specs=in_specs, out_specs=out_specs, check_vma=False)
```

time: 33.4 us -> 21.7 us (0.65)
  Pallas kernels: 32.6 us -> 20.9 us
    pallas_call x1, Pallas kernels: 27.2 us -> 16.1 us  [local(): pl.pallas_call(functools.partial(exchange_kernel, n_shard, n_model, tile)...]
    pallas_call x1, Pallas kernels: 5.42 us -> 4.86 us  [local(): pl.pallas_call(functools.partial(scale_kernel, tuple(plan)), out_shape=[j...]
where the time goes in v2:
time: 21.7 us; the launch traced here: 21.6 us
  Pallas kernels  20.9 us (96%)
  between operations  0.64 us (3%)
    pallas_call x1, Pallas kernels, local(): pl.pallas_call(functools.partial(exchange_kernel, n_shard, n_model, tile)...  16.1 us
    pallas_call x1, Pallas kernels, local(): pl.pallas_call(functools.partial(scale_kernel, tuple(plan)), out_shape=[j...  4.86 us

profile of v2, /device:TPU:0, one launch (start us, length us, event | category | flops | bytes accessed | tf_op | source)
XLA Modules:
  0.0 21.6 jit_solution(1657321071858887787)
XLA Ops:
  0.6 16.1 %exchange.1 = (f32[4096,1024]{1,0:T(8,128)S(1)}, f32[4096,256]{1,0:T(8,128)S(1)}, f32[4096,256]{1,0:T(8,128)S(1)}, f32[1,1024]{1,0:T(1,128)S(1)}, f32[1,256]{1,0...) custom-call(bf16[2048,1024]{1,0:T(8,128)(2,1)} %tq.1, bf16[16,2048]{1,0:T(8,128)(2,1)} %bitcast.9, ...), custom_call_target="tpu_custom_call" | custom-call | bytes 41943040 | tf_op jit(solution)/shard_map/exchange/pallas_call | solution.py:200
  16.7 4.9 %scale.1 = (bf16[4096,1024]{1,0:T(8,128)(2,1)}, bf16[4096,256]{1,0:T(8,128)(2,1)}, bf16[4096,256]{1,0:T(8,128)(2,1)}, f32[1,1024]{1,0:T(1,128)}, f32[1,256]{1,0:...) custom-call(f32[4096,1024]{1,0:T(8,128)S(1)} %get-tuple-element.21.wq, f32[4096,256]{1,0:T(8,128)S(1)} %get-tuple-element.22.wk, ...), custom_call_target="tpu_custom_call" | custom-call | bytes 41943040 | tf_op jit(solution)/shard_map/scale/pallas_call | solution.py:228
